TPU v7x, 32 devices: a whole 2x2x4 slice. The times are simulated.
32 devices in a mesh: lat: 8 (over y, x, core), lon: 4 (over z).
Axes of the slice: x: 2, y: 2, z: 4, core: 2. Of those that a mesh axis runs over, the one named last changes fastest.
Arguments:
- right_side: float32 [128, 2560], P('lat', 'lon'), may hold values from -34 to 34
- first_guess: float32 [128, 2560], P('lat', 'lon'), may hold values from -3 to 3
- cell_mask: int32 [128, 2560], P('lat', 'lon'), may hold values 0 or 1
- cond_east: float32 [128, 2560], P('lat', 'lon'), may hold values from 0.5 to 2
- cond_north: float32 [128, 2560], P('lat', 'lon'), may hold values from 0.5 to 2
- surface: float32 [128, 2560], P('lat', 'lon'), may hold values from 0.02 to 0.5
- recycled: float32 [16, 128, 2560], P(None, 'lat', 'lon'), may hold values from -0.0031444706 to 0.0031444706
Outputs:
- solution: float32 [128, 2560], P('lat', 'lon')
- residual: float32 [128, 2560], P('lat', 'lon')
All inputs are finite; a program needn't handle non-finite values. No bound on the sum of `cell_mask` on one device may be relied on, other than what follows from the above.
Results may differ from a plain program's by a relative error of at most 0.0003.
Values sent between devices are 32-bit elements; how exact they have to be, the bound alone decides.
No kernel may reach another device: no remote copies, remote signals or barrier semaphores. Data moves between devices by JAX's collectives and lax.ppermute only.
A program may use at most 64 MiB of HBM per device.

v0:
```python
import jax
import jax.numpy as jnp
from jax import lax
from jax.experimental import pallas as pl
from jax.experimental.pallas import tpu as pltpu
from jax.sharding import PartitionSpec as P

SHIFT = 5.0
ITERS = 3
DEPTH = ITERS + 1
LANES = 128


def ring(count, step):
    return [(i, (i + step) % count) for i in range(count)]


def pack_kernel(
    basis_hbm, guess_hbm, rhs_hbm, mask_hbm, east_hbm, north_hbm, surf_hbm,
    basis, sides, mask, to_n, to_s, to_e, to_w, sems,
):
    vectors, rows, cols = basis.shape
    moves = [(basis_hbm, basis), (mask_hbm, mask)]
    sources = (guess_hbm, rhs_hbm, east_hbm, north_hbm, surf_hbm)
    moves += [(source, sides.at[i]) for i, source in enumerate(sources)]
    copies = [pltpu.make_async_copy(a, b, sems.at[i]) for i, (a, b) in enumerate(moves)]
    for copy in copies:
        copy.start()
    for copy in copies:
        copy.wait()
    fields = [basis.at[k] for k in range(vectors)]
    fields += [sides.at[0], sides.at[1], mask, sides.at[2], sides.at[3], sides.at[4]]
    strip_e = jnp.zeros((rows, LANES), jnp.float32)
    strip_w = jnp.zeros((rows, LANES), jnp.float32)
    lane = lax.broadcasted_iota(jnp.int32, (rows, LANES), 1)
    for f, ref in enumerate(fields):
        at = DEPTH * f
        to_n[pl.ds(at, DEPTH), :] = ref[rows - DEPTH :, :].astype(jnp.float32)
        to_s[pl.ds(at, DEPTH), :] = ref[:DEPTH, :].astype(jnp.float32)
        here = (lane >= at) & (lane < at + DEPTH)
        last = ref[:, cols - LANES :].astype(jnp.float32)
        first = ref[:, :LANES].astype(jnp.float32)
        strip_e = jnp.where(here, pltpu.roll(last, (at + DEPTH) % LANES, 1), strip_e)
        strip_w = jnp.where(here, pltpu.roll(first, at, 1), strip_w)
    to_e[...] = strip_e
    to_w[...] = strip_w


def roll_lanes(v, by):
    return pltpu.roll(v, by % v.shape[1], 1)


def roll_rows(v, by):
    return pltpu.roll(v, by % v.shape[0], 0)


def apply_faces(v, faces, shift=0.0):
    centre, k_east, k_west, k_north, k_south = faces
    beside = k_east * roll_lanes(v, -1) + k_west * roll_lanes(v, 1)
    above = k_north * roll_rows(v, -1) + k_south * roll_rows(v, 1)
    return (centre - shift) * v - (beside + above)


def edges(f, strip_e, strip_w):
    at = DEPTH * f
    lane = lax.broadcasted_iota(jnp.int32, strip_e.shape, 1)
    edge_e = pltpu.roll(strip_e, (-at) % LANES, 1)
    edge_w = pltpu.roll(strip_w, (LANES - DEPTH - at) % LANES, 1)
    return jnp.where(lane < DEPTH, edge_e, jnp.where(lane >= LANES - DEPTH, edge_w, 0.0))


def faces_of(wet, east, north, surf):
    k_east = east * wet * roll_lanes(wet, -1)
    k_north = north * wet * roll_rows(wet, -1)
    k_west = roll_lanes(k_east, 1)
    k_south = roll_rows(k_north, 1)
    centre = surf * wet + k_east + k_west + k_north + k_south + (1.0 - wet)
    return centre, k_east, k_west, k_north, k_south


def spread_faces(side, faces, q, row):
    for c in range(4):
        line = side[c, row : row + 1, :]
        spread = jnp.broadcast_to(line, (8, line.shape[1]))
        faces[c, q] = spread
        if c == 0:
            faces[4, q] = spread - SHIFT


def power_rows(powers, faces, power, q, vectors):
    source = slice(power * vectors, (power + 1) * vectors)
    target = slice((power + 1) * vectors, (power + 2) * vectors)

    def coefficient(c, q):
        return jnp.concatenate([faces[c, q]] * (vectors // 8), axis=0)

    v = powers[q, source, :]
    beside = coefficient(1, q) * roll_lanes(v, -1) + coefficient(2, q) * roll_lanes(v, 1)
    above = coefficient(3, q) * powers[q + 1, source, :]
    above += coefficient(3, q - 1) * powers[q - 1, source, :]
    middle = coefficient(0 if power == 0 else 4, q)
    powers[q, target, :] = middle * v - (beside + above)


def keep_start_powers(v, faces, rows, start_powers):
    tiles = start_powers.shape[0]
    for power in range(ITERS + 1):
        for tile in range(tiles):
            part = v[:rows, tile * LANES : (tile + 1) * LANES]
            start_powers[tile, pl.ds(power * rows, rows), :] = part
        if power < ITERS:
            v = apply_faces(v, faces, SHIFT)
    spare = (8 - (ITERS + 1)) * rows
    start_powers[:, pl.ds((ITERS + 1) * rows, spare), :] = jnp.zeros(
        (tiles, spare, LANES), jnp.float32
    )


def products(powers, start_powers, batches, rows):
    tiles = start_powers.shape[0]
    nt = (((1,), (1,)), ((), ()))
    total = 0.0
    for batch in batches:
        x = []
        for r in batch:
            tail = [start_powers[t, pl.ds(r, 8, stride=rows), :] for t in range(tiles)]
            tail = jnp.concatenate(tail, axis=1)
            x.append(jnp.concatenate([powers[r + DEPTH, :, : tiles * LANES], tail], axis=0))
        x = jnp.concatenate(x, axis=1)
        high = x.astype(jnp.bfloat16)
        low = (x - high.astype(jnp.float32)).astype(jnp.bfloat16)
        both = jnp.concatenate([high, low], axis=0)
        total += lax.dot_general(both, high, nt, preferred_element_type=jnp.float32)
    return total


def inner_kernel(
    basis, sides, mask, from_e, from_w,
    powers, basis_ext, sums, side, faces, start_powers,
):
    vectors, rows, cols = basis.shape
    tall = rows + 2 * DEPTH
    tiles = cols // LANES
    strip_e, strip_w = from_e[...], from_w[...]
    for k in range(vectors):
        for tile in range(tiles):
            basis_ext[tile, pl.ds(tall * k, rows), :] = basis[k, :, tile * LANES : (tile + 1) * LANES]
        basis_ext[tiles, pl.ds(tall * k, rows), :] = edges(k, strip_e, strip_w)
    own = (sides[0], sides[1], mask[...].astype(jnp.float32), sides[2], sides[3], sides[4])
    guess, rhs, wet, east, north, surf = [
        jnp.concatenate([v, edges(vectors + f, strip_e, strip_w)], axis=1)
        for f, v in enumerate(own)
    ]
    for c, values in enumerate(faces_of(wet, east, north, surf)):
        side[c] = values
    for row in range(rows):
        spread_faces(side, faces, row + DEPTH, row)
        for tile in range(tiles + 1):
            part = basis_ext[tile, pl.ds(row, vectors, stride=tall), :]
            powers[row + DEPTH, :vectors, tile * LANES : (tile + 1) * LANES] = part
    whole = [side[c] for c in range(5)]
    keep_start_powers(rhs - apply_faces(guess, whole), whole, rows, start_powers)
    for power in range(DEPTH):
        first, last = DEPTH + 1 + power, DEPTH + rows - 1 - power
        unroll = (last - first) // (2 if power < 2 else 1)

        def some_rows(i, carry, power=power, first=first, unroll=unroll):
            for u in range(unroll):
                power_rows(powers, faces, power, first + i * unroll + u, vectors)
            return carry

        lax.fori_loop(0, (last - first) // unroll, some_rows, 0)
    middle = range(DEPTH, rows - DEPTH)
    batches = [middle[at : at + DEPTH] for at in range(0, len(middle), DEPTH)]
    sums[...] = products(powers, start_powers, batches, rows)


def outer_kernel(
    inside, basis_in, powers_in, sums, sides, mask,
    from_n, from_s, from_e, from_w, corner_n, corner_s,
    copies, basis_ext, powers, side_ext, fields_ext, faces, start_powers,
):
    del basis_in, powers_in
    rows, cols = mask.shape
    wide = cols + LANES
    tall = rows + 2 * DEPTH
    tiles = cols // LANES
    vectors = basis_ext.shape[1] // tall
    halo_e = jnp.concatenate([corner_n[:DEPTH, :], corner_s[rows - DEPTH : rows, :]], axis=0)
    halo_w = [corner_n[rows : rows + DEPTH, :], corner_s[2 * rows - DEPTH :, :]]
    halo_w = jnp.concatenate(halo_w, axis=0)
    strip_e = jnp.concatenate([from_e[...], halo_e], axis=0)
    strip_w = jnp.concatenate([from_w[...], halo_w], axis=0)

    for k in range(vectors):
        at, to = DEPTH * k, tall * k + rows
        for tile in range(tiles):
            part = pl.ds(tile * LANES, LANES)
            both = [from_n[pl.ds(at, DEPTH), part], from_s[pl.ds(at, DEPTH), part]]
            basis_ext[tile, pl.ds(to, 2 * DEPTH), :] = jnp.concatenate(both, axis=0)
        basis_ext[tiles, pl.ds(to, 2 * DEPTH), :] = edges(k, halo_e, halo_w)
    own = (sides.at[0], sides.at[1], mask, sides.at[2], sides.at[3], sides.at[4])
    for f, ref in enumerate(own):
        at = DEPTH * (vectors + f)
        fields_ext[f, :rows, :cols] = ref[...].astype(jnp.float32)
        fields_ext[f, rows : rows + DEPTH, :cols] = from_n[pl.ds(at, DEPTH), :]
        fields_ext[f, rows + DEPTH :, :cols] = from_s[pl.ds(at, DEPTH), :]
        fields_ext[f, :, cols:] = edges(vectors + f, strip_e, strip_w)
    wet_halo = fields_ext[2, rows:, :] * jnp.concatenate([inside[...]] * (wide // LANES), axis=1)
    wet = jnp.concatenate([fields_ext[2, :rows, :], wet_halo], axis=0)
    for c, values in enumerate(faces_of(wet, fields_ext[3], fields_ext[4], fields_ext[5])):
        side_ext[c] = values

    for q in range(tall):
        ring_row = (q - DEPTH) % tall
        if q <= 2 * DEPTH or q >= rows - 2:
            spread_faces(side_ext, faces, q, ring_row)
        if ring_row >= rows:
            for tile in range(tiles + 1):
                part = basis_ext[tile, pl.ds(ring_row, vectors, stride=tall), :]
                powers[q, :vectors, tile * LANES : (tile + 1) * LANES] = part
    whole = [side_ext[c] for c in range(5)]
    start = fields_ext[1] - apply_faces(fields_ext[0], whole)
    side_ext[5] = start
    keep_start_powers(start, whole, rows, start_powers)
    for power in range(DEPTH):
        for u in range(DEPTH):
            power_rows(powers, faces, power, 1 + power + u, vectors)
            power_rows(powers, faces, power, tall - 2 - power - u, vectors)
    ends = [range(DEPTH), range(rows - DEPTH, rows)]
    both = products(powers, start_powers, ends, rows) + sums[...]
    base = (ITERS + 2) * vectors
    count = base + 8
    full = both[:count] + both[count:] + both[count:].T
    full = jnp.concatenate([full, jnp.zeros((count, LANES - count), jnp.float32)], axis=1)
    at = lax.broadcasted_iota(jnp.int32, (vectors, LANES), 1)
    slabs = [full[a * vectors : (a + 1) * vectors, :] for a in range(4)]
    tail = jnp.concatenate([full[base:, :], jnp.zeros((vectors - 8, LANES), jnp.float32)], axis=0)
    out = jnp.zeros((vectors, LANES), jnp.float32)

    def move(out, v, first, width, target):
        moved = pltpu.roll(v, (target - first) % LANES, 1)
        return jnp.where((at >= target) & (at < target + width), moved, out)

    out = move(out, slabs[0], vectors, vectors, 0)
    out = move(out, slabs[1], vectors, 2 * vectors, vectors)
    out = move(out, slabs[2], 2 * vectors, 2 * vectors, 3 * vectors)
    out = move(out, slabs[3], 3 * vectors, 2 * vectors, 5 * vectors)
    sub = lax.broadcasted_iota(jnp.int32, (vectors, LANES), 0)
    inner_lane = at % vectors
    diagonals = jnp.sum(jnp.where(inner_lane == sub, out, 0.0), axis=0, keepdims=True)
    shared = jnp.where(inner_lane >= sub, out, roll_lanes(out, -vectors))
    merged = out
    for t in range(1, 4):
        merged = move(merged, shared, (2 * t - 1) * vectors, vectors, t * vectors)
    half = vectors // 2
    folded = jnp.where(at[:half] < LANES // 2, merged[:half], roll_lanes(merged[half:], LANES // 2))
    first_lane = at[:1]
    with_start = jnp.zeros((1, LANES), jnp.float32)
    last_line = jnp.where(first_lane < 7 * vectors, diagonals, 0.0)
    for a in range(4):
        line = tail[a : a + 1]
        to, width = 2 * a * vectors, (1 if a == 3 else 2) * vectors
        moved = roll_lanes(line, to - a * vectors)
        with_start = jnp.where((first_lane >= to) & (first_lane < to + width), moved, with_start)
        if a < ITERS:
            to = 7 * vectors + 2 * a
            moved = roll_lanes(line, to - (base + a))
            last_line = jnp.where((first_lane >= to) & (first_lane < to + 2), moved, last_line)
    pieces = [folded[2 * i : 2 * i + 2] for i in range(half // 2)]
    pieces.append(jnp.concatenate([with_start, last_line], axis=0))
    packed = jnp.concatenate(pieces, axis=1)

    def one_copy(device, carry):
        copies[device] = packed
        return carry

    lax.fori_loop(0, copies.shape[0], one_copy, 0, unroll=8)


def finish_kernel(parts, sides, basis_ext, side_ext, solution, residual, spread):
    _, tall, wide = side_ext.shape
    _, rows, cols = sides.shape
    vectors = basis_ext.shape[1] // tall
    free = 7 * vectors
    several = 8

    def add_parts(i, sums):
        return tuple(sums[n] + parts[i * several + n] for n in range(several))

    nothing = (jnp.zeros(parts.shape[1:], jnp.float32),) * several
    sums = list(lax.fori_loop(0, parts.shape[0] // several, add_parts, nothing, unroll=2))
    while len(sums) > 1:
        sums = [sums[i] + sums[i + 1] for i in range(0, len(sums), 2)]
    total = sums[0]
    lane = lax.broadcasted_iota(jnp.int32, (vectors, LANES), 1)
    sub = lax.broadcasted_iota(jnp.int32, (vectors, LANES), 0)
    count = vectors // 4
    folded = jnp.concatenate([total[:, i * LANES : (i + 1) * LANES] for i in range(count)], axis=0)
    with_start = total[:1, count * LANES :]
    last_line = total[1:, count * LANES :]
    merged = jnp.concatenate([folded, roll_lanes(folded, LANES // 2)], axis=0)
    turned = jnp.concatenate([merged] * (LANES // vectors), axis=0).T
    columns_of = jnp.broadcast_to(with_start, (LANES, LANES)).T
    inner_lane = lane % vectors
    table = jnp.where(lane < vectors, merged, 0.0)
    for t in range(1, 4):
        flipped = turned[t * vectors : (t + 1) * vectors]
        upper = jnp.where(inner_lane >= sub, merged, flipped)
        lower = jnp.where(inner_lane < sub, merged, flipped)
        for values, block in ((upper, 2 * t - 1), (lower, 2 * t)):
            moved = roll_lanes(values, (block - t) * vectors)
            table = jnp.where(lane // vectors == block, moved, table)
    even_block = (lane // vectors) % 2 == 0
    fix = (inner_lane == sub) & even_block & (lane >= vectors) & (lane < free)
    table = jnp.where(fix, last_line, table)
    for i in range(7):
        table = jnp.where(lane == free + i, columns_of[i * vectors : (i + 1) * vectors], table)
    total = table
    columns = [jnp.broadcast_to(total[:, i : i + 1], total.shape) for i in range(vectors)]

    def row_of(values, i):
        return jnp.broadcast_to(values[i : i + 1, :], values.shape)

    for i in range(vectors):
        column = columns[i]
        inverse = 1.0 / row_of(column, i)

        def eliminate(values):
            pivot_row = row_of(values, i) * inverse
            return jnp.where(sub == i, pivot_row, values - column * pivot_row)

        columns[i + 1 :] = [eliminate(values) for values in columns[i + 1 :]]
        table = eliminate(table)
    own_lane = (lane % vectors) == sub
    z = [-table[:, free : free + 1]]
    sums = jnp.zeros((vectors, LANES), jnp.float32)
    history = jnp.zeros((1, LANES), jnp.float32)
    lane_row = lane[:1, :]
    for j in range(2 * ITERS):
        newest = jnp.sum(jnp.where(own_lane, z[j], 0.0), axis=0, keepdims=True)
        history = pltpu.roll(history, vectors, 1)
        history = jnp.where((lane_row >= vectors) & (lane_row < 2 * vectors), newest, history)
        terms = (lane >= vectors) & (lane < (j + 2) * vectors)
        weights = jnp.where(terms, history, jnp.where(lane == free + 1 + j, 1.0, 0.0))
        z.append(-jnp.sum(table * weights, axis=1, keepdims=True))
    for j in range(2 * ITERS + 1):
        sums = sums + pltpu.roll(jnp.where(lane >= free, total, 0.0) * z[j], j, 1)
    picked = jnp.where((lane > free) & (lane < free + 7), sums, 0.0)
    moment_row = jnp.sum(picked, axis=0, keepdims=True)
    moment_row += jnp.where(lane_row > free, roll_lanes(last_line, 1), 0.0)
    mu = [moment_row[:, free + 1 + k : free + 2 + k] for k in range(2 * ITERS)]
    for i in range(ITERS + 1):
        spread[i] = jnp.broadcast_to(z[i], (vectors, LANES))

    nil = jnp.zeros((1, 1), jnp.float32)
    rho = [nil + 1.0] + [nil] * ITERS
    gamma = [nil] * (ITERS + 1)
    delta = [nil] * ITERS
    curv = nil
    prev = nil
    for j in range(ITERS):
        norm = nil
        image = nil
        for a in range(j + 1):
            for b in range(j + 1):
                pair = rho[a] * rho[b]
                norm += pair * mu[a + b]
                image += pair * (mu[a + b + 1] + SHIFT * mu[a + b])
        if j == 0:
            gamma = list(rho)
            curv = image
        else:
            ratio = norm / prev
            gamma = [rho[i] + ratio * gamma[i] for i in range(ITERS + 1)]
            curv = image - ratio * ratio * curv
        step = norm / curv
        delta = [delta[i] + step * gamma[i] for i in range(ITERS)]
        below = [nil] + gamma[:ITERS]
        rho = [rho[i] - step * (SHIFT * gamma[i] + below[i]) for i in range(ITERS + 1)]
        prev = norm

    along = [[] for _ in range(ITERS + 1)]
    for tile in range(wide // LANES):
        acc = [jnp.zeros((tall, LANES), jnp.float32) for _ in range(ITERS + 1)]
        for k in range(vectors):
            w = basis_ext[tile, pl.ds(tall * k, tall), :]
            for i in range(ITERS + 1):
                acc[i] = acc[i] + w * spread[i, pl.ds(k, 1), :]
        for i in range(ITERS + 1):
            along[i].append(acc[i])
    along = [jnp.concatenate(pieces, axis=1) for pieces in along]
    faces = [side_ext[c] for c in range(5)]
    v = side_ext[5] + apply_faces(along[0], faces)
    x = sides[0] - along[0][:rows, :cols]
    r = rho[0] * v[:rows, :cols]
    for i in range(ITERS):
        x = x + delta[i] * (v + along[i + 1])[:rows, :cols]
        v = apply_faces(v, faces, SHIFT) + apply_faces(along[i + 1], faces)
        r = r + rho[i + 1] * v[:rows, :cols]
    solution[...] = x
    residual[...] = r


def call(kernel, out_shape, spaces, inputs, scratch=(), flops=10**6, aliases={}):
    return pl.pallas_call(
        kernel,
        out_shape=out_shape,
        in_specs=[pl.BlockSpec(memory_space=space) for space in spaces],
        out_specs=[pl.BlockSpec(memory_space=pltpu.VMEM)] * len(out_shape),
        scratch_shapes=scratch,
        input_output_aliases=aliases,
        cost_estimate=pl.CostEstimate(flops=flops, bytes_accessed=10**6, transcendentals=0),
        compiler_params=pltpu.CompilerParams(vmem_limit_bytes=24 * 1024 * 1024),
    )(*inputs)


def f32(*shape):
    return jax.ShapeDtypeStruct(shape, jnp.float32)


def shards(right_side, first_guess, cell_mask, cond_east, cond_north, surface, recycled):
    vectors, rows, cols = recycled.shape
    n_lat, n_lon = lax.axis_size("lat"), lax.axis_size("lon")
    devices = n_lat * n_lon
    fields = vectors + 6
    tall, wide = rows + 2 * DEPTH, cols + LANES
    tiles = cols // LANES
    own = (recycled, first_guess, right_side, cell_mask, cond_east, cond_north, surface)
    band, strip = f32(fields * DEPTH, cols), f32(rows, LANES)
    basis, sides, mask, to_n, to_s, to_e, to_w = call(
        pack_kernel,
        [f32(vectors, rows, cols), f32(5, rows, cols), jax.ShapeDtypeStruct((rows, cols), jnp.int32)]
        + [band, band, strip, strip],
        [pltpu.HBM] * 7,
        [pltpu.with_memory_space_constraint(array, pltpu.HBM) for array in own],
        scratch=[pltpu.SemaphoreType.DMA((7,))],
    )
    north, south = ring(n_lat, 1), ring(n_lat, -1)
    from_w = lax.ppermute(to_e, "lon", ring(n_lon, 1))
    from_e = lax.ppermute(to_w, "lon", ring(n_lon, -1))
    from_s = lax.ppermute(to_n, "lat", north)
    from_n = lax.ppermute(to_s, "lat", south)
    strips = jnp.concatenate([from_e, from_w], axis=0)
    corner_s = lax.ppermute(strips, "lat", north)
    corner_n = lax.ppermute(strips, "lat", south)
    here = lax.axis_index("lat")
    inside = jnp.stack([here < n_lat - 1, here > 0]).astype(jnp.float32)
    inside = jnp.broadcast_to(inside[:, None, None], (2, DEPTH, LANES)).reshape(-1, LANES)
    count = (ITERS + 2) * vectors
    powers = f32(tall, count, wide)
    basis_ext = f32(tiles + 1, vectors * tall, LANES)
    faces = pltpu.VMEM((5, tall, 8, wide), jnp.float32)
    start_powers = pltpu.VMEM((tiles, 8 * rows, LANES), jnp.float32)
    powers, basis_ext, sums = call(
        inner_kernel,
        [powers, basis_ext, f32(2 * (count + 8), count + 8)],
        [pltpu.VMEM] * 5,
        (basis, sides, mask, from_e, from_w),
        scratch=[pltpu.VMEM((5, rows, wide), jnp.float32), faces, start_powers],
        flops=10**9,
    )
    copies, basis_ext, _, side_ext = call(
        outer_kernel,
        [f32(devices, 2, (vectors // 4 + 1) * LANES), basis_ext, powers, f32(6, tall, wide)],
        [pltpu.VMEM] * 12,
        (inside, basis_ext, powers, sums, sides, mask)
        + (from_n, from_s, from_e, from_w, corner_n, corner_s),
        scratch=[pltpu.VMEM((6, tall, wide), jnp.float32), faces, start_powers],
        aliases={1: 1, 2: 2},
    )
    parts = lax.all_to_all(copies, ("lat", "lon"), 0, 0)
    return call(
        finish_kernel,
        [f32(rows, cols), f32(rows, cols)],
        [pltpu.VMEM] * 4,
        (parts, sides, basis_ext, side_ext),
        scratch=[pltpu.VMEM((ITERS + 1, vectors, LANES), jnp.float32)],
    )


def solution(mesh):
    block = P("lat", "lon")
    return jax.shard_map(
        shards,
        mesh=mesh,
        in_specs=(block,) * 6 + (P(None, "lat", "lon"),),
        out_specs=(block, block),
        check_vma=False,
    )
```

profile of v0, /device:TPU:0, one launch (start us, length us, event | category | flops | bytes accessed | tf_op | source)
XLA Modules:
  0.0 34.5 jit_solution(1825673936005946616)
XLA Ops:
  0.6 1.4 %shard_map.86 = (f32[16,16,640]{2,1,0:T(8,128)S(1)}, f32[5,16,640]{2,1,0:T(8,128)S(1)}, s32[16,640]{1,0:T(8,128)S(1)}, f32[88,640]{1,0:T(8,128)S(1)}, f32[88,640...) custom-call(f32[16,16,640]{2,1,0:T(8,128)} %basis_hbm.1, f32[16,640]{1,0:T(8,128)} %guess_hbm.1, ...), custom_call_target="tpu_custom_call" | custom-call | flops 1000000 | bytes 1000000 | tf_op jit(solution)/shard_map/pallas_call | solution.py:406
  2.0 5.1 %collective-permute-start = (f32[16,128]{1,0:T(8,128)S(1)}, f32[16,128]{1,0:T(8,128)S(1)}, u32[]{:S(2)}, u32[]{:S(2)}) collective-permute-start(f32[16,128]{1,0:T(8,128)S(1)} %get-tuple-element.18), channel_id=1, source_target_pairs={{0,3},{1,0},{2,1},{3,2},{4,7},{5,4},{6,5},{7,6},{8,11},{9,8},{10,9... | collective-permute-start | bytes 24584 | tf_op jit(solution)/shard_map/ppermute | solution.py:441
  7.2 0.0 collective-permute-start.1
  7.2 1.6 %collective-permute-start.2 = (f32[88,640]{1,0:T(8,128)S(1)}, f32[88,640]{1,0:T(8,128)S(1)}, u32[]{:S(2)}, u32[]{:S(2)}) collective-permute-start(f32[88,640]{1,0:T(8,128)S(1)} %get-tuple-element.23), channel_id=1, source_target_pairs={{0,28},{4,0},{8,4},{12,8},{16,12},{20,16},{24,20},{28,24},{1,29},{... | collective-permute-start | bytes 675848 | tf_op jit(solution)/shard_map/ppermute | solution.py:443
  8.8 0.0 collective-permute-start.3
  8.8 0.1 add_convert_fusion
  8.9 0.1 broadcast_in_dim.10
  8.9 0.1 broadcast_in_dim.11
  9.0 0.0 collective-permute-done.from_e
  9.0 3.6 %collective-permute-done.1.from_w = f32[16,128]{1,0:T(8,128)S(1)} collective-permute-done((f32[16,128]{1,0:T(8,128)S(1)}, f32[16,128]{1,0:T(8,128)S(1)}, u32[]{:S(2)}, u32[]{:S(2)}) %collective-permute-start.1) | collective-permute-done | bytes 8224 | tf_op jit(solution)/shard_map/ppermute | solution.py:440
  12.6 0.0 collective-permute-start.5
  12.6 2.6 %collective-permute-start.4 = (f32[32,128]{1,0:T(8,128)S(1)}, f32[32,128]{1,0:T(8,128)S(1)}, u32[]{:S(2)}, u32[]{:S(2)}) collective-permute-start(f32[32,128]{1,0:T(8,128)S(1)} %constant_dynamic-update-slice_fusion), channel_id=1, source_target_pairs={{0,28},{4,0},{8,4},{12,8},{16,12},{20,16},{24,20},{28,24},{1,29},{... | collective-permute-start | bytes 49160 | tf_op jit(solution)/shard_map/ppermute | solution.py:446
  15.3 2.8 %shard_map.87 = (f32[24,80,768]{2,1,0:T(8,128)S(1)}, f32[6,384,128]{2,1,0:T(8,128)S(1)}, f32[176,88]{1,0:T(8,128)S(1)}) custom-call(f32[16,16,640]{2,1,0:T(8,128)S(1)} %get-tuple-element.15.basis, f32[5,16,640]{2,1,0:T(8,128)S(1)} %get-tuple-element.16.sides, s32[16,640]{1,0:T(8,128)S(1)} %get-tuple-element.17.mask, ...), custom_call_target="tpu_custom_call" | custom-call | flops 1000000000 | bytes 1000000 | tf_op jit(solution)/shard_map/pallas_call | solution.py:406
  18.1 0.0 collective-permute-done.5.corner_s
  18.1 0.0 collective-permute-done.4.corner_n
  18.1 0.0 collective-permute-done.2.from_n
  18.1 0.0 collective-permute-done.3.from_s
  18.2 0.1 broadcast_in_dim.12.inside
  18.2 2.4 %shard_map.88 = (f32[32,2,640]{2,1,0:T(2,128)S(1)}, f32[6,384,128]{2,1,0:T(8,128)S(1)}, f32[24,80,768]{2,1,0:T(8,128)S(1)}, f32[6,24,768]{2,1,0:T(8,128)S(1)}) custom-call(f32[8,128]{1,0:T(8,128)S(1)} %broadcast_in_dim.12.inside, f32[6,384,128]{2,1,0:T(8,128)S(1)} %get-tuple-element.20.basis_in, ...), custom_call_target="tpu_custom_call", output_to_operand_aliasing={{1}: (1, {}), {2}: (2, {})} | custom-call | flops 1000000 | bytes 1000000 | tf_op jit(solution)/shard_map/pallas_call | solution.py:406
  20.7 11.3 %all_to_all.5.parts = f32[32,2,640]{2,1,0:T(2,128)S(1)} all-to-all(f32[32,2,640]{2,1,0:T(2,128)S(1)} %get-tuple-element.25), channel_id=1, replica_groups=mesh['lat'=8,'lon'=4] {'lat','lon'}, dimensions={0} | all-to-all | bytes 327680 | tf_op jit(solution)/shard_map/all_to_all | solution.py:472
  32.0 2.5 %shard_map.89 = (f32[16,640]{1,0:T(8,128)}, f32[16,640]{1,0:T(8,128)}) custom-call(f32[32,2,640]{2,1,0:T(2,128)S(1)} %all_to_all.5.parts, f32[5,16,640]{2,1,0:T(8,128)S(1)} %get-tuple-element.16.sides, f32[6,384,128]{2,1,0:T(8,128)S(1)} %get-tuple-element.26.basis_ext, f32[6,24,768]{2,1,0:T(8,128)S(1)} %get-tuple-element.27.side_ext), custom_call_target="tpu_custom_call" | custom-call | flops 1000000 | bytes 1000000 | tf_op jit(solution)/shard_map/pallas_call | solution.py:406
  (2 shorter events, 0.0 us)
Async XLA Ops:
  2.0 7.0 %collective-permute-start = (f32[16,128]{1,0:T(8,128)S(1)}, f32[16,128]{1,0:T(8,128)S(1)}, u32[]{:S(2)}, u32[]{:S(2)}) collective-permute-start(f32[16,128]{1,0:T(8,128)S(1)} %get-tuple-element.18), channel_id=1, source_target_pairs={{0,3},{1,0},{2,1},{3,2},{4,7},{5,4},{6,5},{7,6},{8,11},{9,8},{10,9... | collective-permute-start | bytes 24584 | tf_op jit(solution)/shard_map/ppermute | solution.py:441
  7.2 5.4 %collective-permute-start.1 = (f32[16,128]{1,0:T(8,128)S(1)}, f32[16,128]{1,0:T(8,128)S(1)}, u32[]{:S(2)}, u32[]{:S(2)}) collective-permute-start(f32[16,128]{1,0:T(8,128)S(1)} %get-tuple-element.19), channel_id=1, source_target_pairs={{0,1},{1,2},{2,3},{3,0},{4,5},{5,6},{6,7},{7,4},{8,9},{9,10},{10,1... | collective-permute-start | bytes 24584 | tf_op jit(solution)/shard_map/ppermute | solution.py:440
  7.2 11.0 %collective-permute-start.2 = (f32[88,640]{1,0:T(8,128)S(1)}, f32[88,640]{1,0:T(8,128)S(1)}, u32[]{:S(2)}, u32[]{:S(2)}) collective-permute-start(f32[88,640]{1,0:T(8,128)S(1)} %get-tuple-element.23), channel_id=1, source_target_pairs={{0,28},{4,0},{8,4},{12,8},{16,12},{20,16},{24,20},{28,24},{1,29},{... | collective-permute-start | bytes 675848 | tf_op jit(solution)/shard_map/ppermute | solution.py:443
  8.8 9.4 %collective-permute-start.3 = (f32[88,640]{1,0:T(8,128)S(1)}, f32[88,640]{1,0:T(8,128)S(1)}, u32[]{:S(2)}, u32[]{:S(2)}) collective-permute-start(f32[88,640]{1,0:T(8,128)S(1)} %get-tuple-element.24), channel_id=1, source_target_pairs={{0,4},{4,8},{8,12},{12,16},{16,20},{20,24},{24,28},{28,0},{1,5},{5... | collective-permute-start | bytes 675848 | tf_op jit(solution)/shard_map/ppermute | solution.py:442
  12.6 5.5 %collective-permute-start.5 = (f32[32,128]{1,0:T(8,128)S(1)}, f32[32,128]{1,0:T(8,128)S(1)}, u32[]{:S(2)}, u32[]{:S(2)}) collective-permute-start(f32[32,128]{1,0:T(8,128)S(1)} %constant_dynamic-update-slice_fusion), channel_id=1, source_target_pairs={{0,4},{4,8},{8,12},{12,16},{16,20},{20,24},{24,28},{28,0},{1,5},{5... | collective-permute-start | bytes 49160 | tf_op jit(solution)/shard_map/ppermute | solution.py:445
  12.6 5.5 %collective-permute-start.4 = (f32[32,128]{1,0:T(8,128)S(1)}, f32[32,128]{1,0:T(8,128)S(1)}, u32[]{:S(2)}, u32[]{:S(2)}) collective-permute-start(f32[32,128]{1,0:T(8,128)S(1)} %constant_dynamic-update-slice_fusion), channel_id=1, source_target_pairs={{0,28},{4,0},{8,4},{12,8},{16,12},{20,16},{24,20},{28,24},{1,29},{... | collective-permute-start | bytes 49160 | tf_op jit(solution)/shard_map/ppermute | solution.py:446
where the time goes:
time: 34.6 us; the launch traced here: 34.5 us
  blocking collectives  11.3 us (33%)
  starting transfers between devices  9.39 us (27%)
  Pallas kernels  9.18 us (27%)
  waiting for transfers between devices  3.61 us (10%)
  between operations  0.69 us (2%)
    all_to_all x1, blocking collectives, shards(): parts = lax.all_to_all(copies, ('lat', 'lon'), 0, 0)  11.3 us
    pallas_call x4, Pallas kernels, call(): pl.pallas_call(kernel, out_shape=out_shape, in_specs=[pl.BlockSpec(memory...  9.18 us
    ppermute x1, starting transfers between devices, shards(): from_e = lax.ppermute(to_w, 'lon', ring(n_lon, -1))  5.13 us
    ppermute x1, waiting for transfers between devices, shards(): from_w = lax.ppermute(to_e, 'lon', ring(n_lon, 1))  3.6 us
    ppermute x1, starting transfers between devices, shards(): corner_n = lax.ppermute(strips, 'lat', south)  2.64 us
    ppermute x1, starting transfers between devices, shards(): from_n = lax.ppermute(to_s, 'lat', south)  1.61 us
  transfers between devices with their start and end apart: 6, of which 1 were waited for; matrix products, arithmetic and copies ran while one was open for 1% of the time, Pallas kernels for 8%

commit v1 on v0

--- a/solution.py
+++ b/solution.py
@@ -130,7 +130,7 @@
         high = x.astype(jnp.bfloat16)
         low = (x - high.astype(jnp.float32)).astype(jnp.bfloat16)
         both = jnp.concatenate([high, low], axis=0)
-        total += lax.dot_general(both, high, nt, preferred_element_type=jnp.float32)
+        total += lax.dot_general(both, both, nt, preferred_element_type=jnp.float32)
     return total
 
 
@@ -231,7 +231,8 @@
     both = products(powers, start_powers, ends, rows) + sums[...]
     base = (ITERS + 2) * vectors
     count = base + 8
-    full = both[:count] + both[count:] + both[count:].T
+    full = both[:count] + both[count:]
+    full = full[:, :count] + full[:, count:]
     full = jnp.concatenate([full, jnp.zeros((count, LANES - count), jnp.float32)], axis=1)
     at = lax.broadcasted_iota(jnp.int32, (vectors, LANES), 1)
     slabs = [full[a * vectors : (a + 1) * vectors, :] for a in range(4)]
@@ -454,7 +455,7 @@
     start_powers = pltpu.VMEM((tiles, 8 * rows, LANES), jnp.float32)
     powers, basis_ext, sums = call(
         inner_kernel,
-        [powers, basis_ext, f32(2 * (count + 8), count + 8)],
+        [powers, basis_ext, f32(2 * (count + 8), 2 * (count + 8))],
         [pltpu.VMEM] * 5,
         (basis, sides, mask, from_e, from_w),
         scratch=[pltpu.VMEM((5, rows, wide), jnp.float32), faces, start_powers],

time: 34.6 us -> 34.5 us (level)
  no operation moved by 1% of the time
where the time goes in v1:
time: 34.5 us; the launch traced here: 34.4 us
  blocking collectives  11.3 us (33%)
  starting transfers between devices  9.39 us (27%)
  Pallas kernels  9.12 us (26%)
  waiting for transfers between devices  3.61 us (10%)
  between operations  0.69 us (2%)
    all_to_all x1, blocking collectives, shards(): parts = lax.all_to_all(copies, ('lat', 'lon'), 0, 0)  11.3 us
    pallas_call x4, Pallas kernels, call(): pl.pallas_call(kernel, out_shape=out_shape, in_specs=[pl.BlockSpec(memory...  9.12 us
    ppermute x1, starting transfers between devices, shards(): from_e = lax.ppermute(to_w, 'lon', ring(n_lon, -1))  5.13 us
    ppermute x1, waiting for transfers between devices, shards(): from_w = lax.ppermute(to_e, 'lon', ring(n_lon, 1))  3.6 us
    ppermute x1, starting transfers between devices, shards(): corner_n = lax.ppermute(strips, 'lat', south)  2.64 us
    ppermute x1, starting transfers between devices, shards(): from_n = lax.ppermute(to_s, 'lat', south)  1.61 us
  transfers between devices with their start and end apart: 6, of which 1 were waited for; matrix products, arithmetic and copies ran while one was open for 1% of the time, Pallas kernels for 8%

profile of v1, /device:TPU:0, one launch (start us, length us, event | category | flops | bytes accessed | tf_op | source)
XLA Modules:
  0.0 34.4 jit_solution(9705755473964587178)
XLA Ops:
  0.6 1.4 %shard_map.86 = (f32[16,16,640]{2,1,0:T(8,128)S(1)}, f32[5,16,640]{2,1,0:T(8,128)S(1)}, s32[16,640]{1,0:T(8,128)S(1)}, f32[88,640]{1,0:T(8,128)S(1)}, f32[88,640...) custom-call(f32[16,16,640]{2,1,0:T(8,128)} %basis_hbm.1, f32[16,640]{1,0:T(8,128)} %guess_hbm.1, ...), custom_call_target="tpu_custom_call" | custom-call | flops 1000000 | bytes 1000000 | tf_op jit(solution)/shard_map/pallas_call | solution.py:407
  2.0 5.1 %collective-permute-start = (f32[16,128]{1,0:T(8,128)S(1)}, f32[16,128]{1,0:T(8,128)S(1)}, u32[]{:S(2)}, u32[]{:S(2)}) collective-permute-start(f32[16,128]{1,0:T(8,128)S(1)} %get-tuple-element.18), channel_id=1, source_target_pairs={{0,3},{1,0},{2,1},{3,2},{4,7},{5,4},{6,5},{7,6},{8,11},{9,8},{10,9... | collective-permute-start | bytes 24584 | tf_op jit(solution)/shard_map/ppermute | solution.py:442
  7.2 0.0 collective-permute-start.1
  7.2 1.6 %collective-permute-start.2 = (f32[88,640]{1,0:T(8,128)S(1)}, f32[88,640]{1,0:T(8,128)S(1)}, u32[]{:S(2)}, u32[]{:S(2)}) collective-permute-start(f32[88,640]{1,0:T(8,128)S(1)} %get-tuple-element.23), channel_id=1, source_target_pairs={{0,28},{4,0},{8,4},{12,8},{16,12},{20,16},{24,20},{28,24},{1,29},{... | collective-permute-start | bytes 675848 | tf_op jit(solution)/shard_map/ppermute | solution.py:444
  8.8 0.0 collective-permute-start.3
  8.8 0.1 add_convert_fusion
  8.9 0.1 broadcast_in_dim.10
  8.9 0.1 broadcast_in_dim.11
  9.0 0.0 collective-permute-done.from_e
  9.0 3.6 %collective-permute-done.1.from_w = f32[16,128]{1,0:T(8,128)S(1)} collective-permute-done((f32[16,128]{1,0:T(8,128)S(1)}, f32[16,128]{1,0:T(8,128)S(1)}, u32[]{:S(2)}, u32[]{:S(2)}) %collective-permute-start.1) | collective-permute-done | bytes 8224 | tf_op jit(solution)/shard_map/ppermute | solution.py:441
  12.6 0.0 collective-permute-start.5
  12.6 2.6 %collective-permute-start.4 = (f32[32,128]{1,0:T(8,128)S(1)}, f32[32,128]{1,0:T(8,128)S(1)}, u32[]{:S(2)}, u32[]{:S(2)}) collective-permute-start(f32[32,128]{1,0:T(8,128)S(1)} %constant_dynamic-update-slice_fusion), channel_id=1, source_target_pairs={{0,28},{4,0},{8,4},{12,8},{16,12},{20,16},{24,20},{28,24},{1,29},{... | collective-permute-start | bytes 49160 | tf_op jit(solution)/shard_map/ppermute | solution.py:447
  15.3 2.9 %shard_map.87 = (f32[24,80,768]{2,1,0:T(8,128)S(1)}, f32[6,384,128]{2,1,0:T(8,128)S(1)}, f32[176,176]{1,0:T(8,128)S(1)}) custom-call(f32[16,16,640]{2,1,0:T(8,128)S(1)} %get-tuple-element.15.basis, f32[5,16,640]{2,1,0:T(8,128)S(1)} %get-tuple-element.16.sides, s32[16,640]{1,0:T(8,128)S(1)} %get-tuple-element.17.mask, ...), custom_call_target="tpu_custom_call" | custom-call | flops 1000000000 | bytes 1000000 | tf_op jit(solution)/shard_map/pallas_call | solution.py:407
  18.2 0.0 collective-permute-done.5.corner_s
  18.2 0.0 collective-permute-done.4.corner_n
  18.2 0.0 collective-permute-done.2.from_n
  18.2 0.0 collective-permute-done.3.from_s
  18.2 0.1 broadcast_in_dim.12.inside
  18.3 2.3 %shard_map.88 = (f32[32,2,640]{2,1,0:T(2,128)S(1)}, f32[6,384,128]{2,1,0:T(8,128)S(1)}, f32[24,80,768]{2,1,0:T(8,128)S(1)}, f32[6,24,768]{2,1,0:T(8,128)S(1)}) custom-call(f32[8,128]{1,0:T(8,128)S(1)} %broadcast_in_dim.12.inside, f32[6,384,128]{2,1,0:T(8,128)S(1)} %get-tuple-element.20.basis_in, ...), custom_call_target="tpu_custom_call", output_to_operand_aliasing={{1}: (1, {}), {2}: (2, {})} | custom-call | flops 1000000 | bytes 1000000 | tf_op jit(solution)/shard_map/pallas_call | solution.py:407
  20.6 11.3 %all_to_all.5.parts = f32[32,2,640]{2,1,0:T(2,128)S(1)} all-to-all(f32[32,2,640]{2,1,0:T(2,128)S(1)} %get-tuple-element.25), channel_id=1, replica_groups=mesh['lat'=8,'lon'=4] {'lat','lon'}, dimensions={0} | all-to-all | bytes 327680 | tf_op jit(solution)/shard_map/all_to_all | solution.py:473
  31.9 2.5 %shard_map.89 = (f32[16,640]{1,0:T(8,128)}, f32[16,640]{1,0:T(8,128)}) custom-call(f32[32,2,640]{2,1,0:T(2,128)S(1)} %all_to_all.5.parts, f32[5,16,640]{2,1,0:T(8,128)S(1)} %get-tuple-element.16.sides, f32[6,384,128]{2,1,0:T(8,128)S(1)} %get-tuple-element.26.basis_ext, f32[6,24,768]{2,1,0:T(8,128)S(1)} %get-tuple-element.27.side_ext), custom_call_target="tpu_custom_call" | custom-call | flops 1000000 | bytes 1000000 | tf_op jit(solution)/shard_map/pallas_call | solution.py:407
  (2 shorter events, 0.0 us)
Async XLA Ops:
  2.0 7.0 %collective-permute-start = (f32[16,128]{1,0:T(8,128)S(1)}, f32[16,128]{1,0:T(8,128)S(1)}, u32[]{:S(2)}, u32[]{:S(2)}) collective-permute-start(f32[16,128]{1,0:T(8,128)S(1)} %get-tuple-element.18), channel_id=1, source_target_pairs={{0,3},{1,0},{2,1},{3,2},{4,7},{5,4},{6,5},{7,6},{8,11},{9,8},{10,9... | collective-permute-start | bytes 24584 | tf_op jit(solution)/shard_map/ppermute | solution.py:442
  7.2 5.4 %collective-permute-start.1 = (f32[16,128]{1,0:T(8,128)S(1)}, f32[16,128]{1,0:T(8,128)S(1)}, u32[]{:S(2)}, u32[]{:S(2)}) collective-permute-start(f32[16,128]{1,0:T(8,128)S(1)} %get-tuple-element.19), channel_id=1, source_target_pairs={{0,1},{1,2},{2,3},{3,0},{4,5},{5,6},{6,7},{7,4},{8,9},{9,10},{10,1... | collective-permute-start | bytes 24584 | tf_op jit(solution)/shard_map/ppermute | solution.py:441
  7.2 11.0 %collective-permute-start.2 = (f32[88,640]{1,0:T(8,128)S(1)}, f32[88,640]{1,0:T(8,128)S(1)}, u32[]{:S(2)}, u32[]{:S(2)}) collective-permute-start(f32[88,640]{1,0:T(8,128)S(1)} %get-tuple-element.23), channel_id=1, source_target_pairs={{0,28},{4,0},{8,4},{12,8},{16,12},{20,16},{24,20},{28,24},{1,29},{... | collective-permute-start | bytes 675848 | tf_op jit(solution)/shard_map/ppermute | solution.py:444
  8.8 9.4 %collective-permute-start.3 = (f32[88,640]{1,0:T(8,128)S(1)}, f32[88,640]{1,0:T(8,128)S(1)}, u32[]{:S(2)}, u32[]{:S(2)}) collective-permute-start(f32[88,640]{1,0:T(8,128)S(1)} %get-tuple-element.24), channel_id=1, source_target_pairs={{0,4},{4,8},{8,12},{12,16},{16,20},{20,24},{24,28},{28,0},{1,5},{5... | collective-permute-start | bytes 675848 | tf_op jit(solution)/shard_map/ppermute | solution.py:443
  12.6 5.6 %collective-permute-start.5 = (f32[32,128]{1,0:T(8,128)S(1)}, f32[32,128]{1,0:T(8,128)S(1)}, u32[]{:S(2)}, u32[]{:S(2)}) collective-permute-start(f32[32,128]{1,0:T(8,128)S(1)} %constant_dynamic-update-slice_fusion), channel_id=1, source_target_pairs={{0,4},{4,8},{8,12},{12,16},{16,20},{20,24},{24,28},{28,0},{1,5},{5... | collective-permute-start | bytes 49160 | tf_op jit(solution)/shard_map/ppermute | solution.py:446
  12.6 5.6 %collective-permute-start.4 = (f32[32,128]{1,0:T(8,128)S(1)}, f32[32,128]{1,0:T(8,128)S(1)}, u32[]{:S(2)}, u32[]{:S(2)}) collective-permute-start(f32[32,128]{1,0:T(8,128)S(1)} %constant_dynamic-update-slice_fusion), channel_id=1, source_target_pairs={{0,28},{4,0},{8,4},{12,8},{16,12},{20,16},{24,20},{28,24},{1,29},{... | collective-permute-start | bytes 49160 | tf_op jit(solution)/shard_map/ppermute | solution.py:447
